TPU v7x, 32 devices: a whole 2x2x4 slice. The times are simulated.
32 devices in a mesh: far: 4 (over z), near: 8 (over y, x, core).
Axes of the slice: x: 2, y: 2, z: 4, core: 2. Of those that a mesh axis runs over, the one named last changes fastest.
Arguments:
- state_real: float32 [4, 8, 2, 128, 128], P('far', 'near'), may hold values from -5 to 5
- state_imag: float32 [4, 8, 2, 128, 128], P('far', 'near'), may hold values from -5 to 5
- gate_real: float32 [2, 4, 3, 128, 128], replicated, may hold values from -0.375 to 0.375
- gate_imag: float32 [2, 4, 3, 128, 128], replicated, may hold values from -0.375 to 0.375
Outputs:
- final_real: float32 [4, 8, 2, 128, 128], P('far', 'near')
- final_imag: float32 [4, 8, 2, 128, 128], P('far', 'near')
All inputs are finite; a program needn't handle non-finite values.
Results may differ from a plain program's by a relative error of at most 0.000071.
Values sent between devices are 32-bit elements; how exact they have to be, the bound alone decides.
A program may use at most 64 MiB of HBM per device.

v0:
```python
import functools

import jax
import jax.numpy as jnp
from jax import lax
from jax.experimental import pallas as pl
from jax.experimental.pallas import tpu as pltpu
from jax.sharding import PartitionSpec as P


def gate_low(x, g):
    return jnp.einsum(
        "...l,jl->...j", x, g, precision=lax.Precision.HIGHEST, preferred_element_type=jnp.float32
    )


def gate_mid(x, g):
    return jnp.einsum(
        "...ml,jm->...jl", x, g, precision=lax.Precision.HIGHEST, preferred_element_type=jnp.float32
    )


def gate_top(x, g):
    high, width, lows = (x.shape[-3], x.shape[-2], x.shape[-1])
    upper = g.shape[0] // high
    lead = x.shape[:-3]
    viewed = x.reshape(lead + (high, upper, width // upper, lows))
    matrix = g.reshape((g.shape[0], high, upper))
    out = jnp.einsum(
        "...hkrl,jhk->...jrl",
        viewed,
        matrix,
        precision=lax.Precision.HIGHEST,
        preferred_element_type=jnp.float32,
    )
    return out.reshape(lead + (high, width, lows))


def complex_gate(form, real, imag, greal, gimag):
    new_real = form(real, greal) - form(imag, gimag)
    new_imag = form(imag, greal) + form(real, gimag)
    return (new_real, new_imag)


def merged_rows(x):
    return x.reshape((1, 1, x.shape[2] * x.shape[3], x.shape[4]))


def on_device(state_real, state_imag, gate_real, gate_imag):
    real, imag = (state_real, state_imag)
    forms = (gate_low, gate_mid, gate_top)
    shape = state_real.shape
    for rnd in range(gate_real.shape[0]):
        for section in range(4):
            if section == 2:
                order = [1, 0, 2]
            else:
                order = [0, 1, 2]
            early = []
            later = order[len(early) :]
            pair = (real, imag)
            if section == 0:
                moved = (
                    lax.all_to_all(
                        merged_rows(pair[0]), "far", split_axis=2, concat_axis=2, tiled=True
                    ),
                    lax.all_to_all(
                        merged_rows(pair[1]), "far", split_axis=2, concat_axis=2, tiled=True
                    ),
                )
                pair = (moved[0].reshape(shape), moved[1].reshape(shape))
            elif section == 1:
                pair = (
                    lax.all_to_all(pair[0], "near", split_axis=3, concat_axis=3, tiled=True),
                    lax.all_to_all(pair[1], "near", split_axis=3, concat_axis=3, tiled=True),
                )
            elif section == 2:
                pair = (
                    lax.all_to_all(pair[0], "near", split_axis=4, concat_axis=4, tiled=True),
                    lax.all_to_all(pair[1], "near", split_axis=4, concat_axis=4, tiled=True),
                )
            else:
                moved = (
                    lax.all_to_all(
                        merged_rows(pair[0]), "near", split_axis=2, concat_axis=2, tiled=True
                    ),
                    lax.all_to_all(
                        merged_rows(pair[1]), "near", split_axis=2, concat_axis=2, tiled=True
                    ),
                )
                pair = (moved[0].reshape(shape), moved[1].reshape(shape))
            for which in later:
                pair = complex_gate(
                    forms[which],
                    pair[0],
                    pair[1],
                    gate_real[rnd, section, which],
                    gate_imag[rnd, section, which],
                )
            real, imag = pair
    return (real, imag)


def parts(x):
    first = x.astype(jnp.bfloat16)
    return first, (x - first.astype(jnp.float32)).astype(jnp.bfloat16)


def dot(a, b, dims):
    def product(x, y):
        return lax.dot_general(x, y, (dims, ((), ())), preferred_element_type=jnp.float32)

    return product(a[0], b[0]) + (product(a[0], b[1]) + product(a[1], b[0]))


def complex_matrix(greal, gimag):
    return jnp.concatenate(
        [jnp.concatenate([greal, -gimag], axis=1), jnp.concatenate([gimag, greal], axis=1)], axis=0
    )


def kernel(sizes, sr_ref, si_ref, gr_hbm, gi_hbm, or_ref, oi_ref, *scratch):
    nfar, nnear, rounds, high, order, lows = sizes
    sections = 4 * rounds
    sends, recvs = scratch[: sections - 1], scratch[sections - 1 : 2 * sections - 1]
    gr_ref, gi_ref, w_ref, x_ref, send_sem, recv_sem, own_sem, gate_sem = scratch[2 * sections - 1 :]
    far, near = lax.axis_index("far"), lax.axis_index("near")
    upper = order // high
    rest = order // upper

    loads = [
        pltpu.make_async_copy(gr_hbm, gr_ref, gate_sem.at[0]),
        pltpu.make_async_copy(gi_hbm, gi_ref, gate_sem.at[1]),
    ]
    for load in loads:
        load.start()
    barrier = pltpu.get_barrier_semaphore()
    for k in range(1, nfar):
        pl.semaphore_signal(
            barrier, inc=1, device_id=(lax.rem(far + k, nfar), near), device_id_type=pl.DeviceIdType.MESH
        )
    for k in range(1, nnear):
        pl.semaphore_signal(
            barrier, inc=1, device_id=(far, lax.rem(near + k, nnear)), device_id_type=pl.DeviceIdType.MESH
        )
    pl.semaphore_wait(barrier, nfar - 1 + nnear - 1)

    pending = []

    def launch(step, c):
        n, me = (nfar, far) if step % 4 == 0 else (nnear, near)
        source = (sr_ref, si_ref)[c] if step == 0 else sends[step - 1].at[c]
        recv = recvs[step].at[c]
        copies = []
        for k in range(1, n):
            to = lax.rem(me + k, n)
            copy = pltpu.make_async_remote_copy(
                src_ref=source.at[to],
                dst_ref=recv.at[me],
                send_sem=send_sem.at[step, c, k],
                recv_sem=recv_sem.at[step, c, k],
                device_id=(to, near) if step % 4 == 0 else (far, to),
                device_id_type=pl.DeviceIdType.MESH,
            )
            copy.start()
            pending.append(copy)
        own = pltpu.make_async_copy(source.at[me], recv.at[me], own_sem.at[step, c])
        own.start()

    def arrive(step, c):
        n, me = (nfar, far) if step % 4 == 0 else (nnear, near)
        recv = recvs[step].at[c]
        pltpu.make_async_copy(recv.at[me], recv.at[me], own_sem.at[step, c]).wait()
        for k in range(1, n):
            origin = lax.rem(me + n - k, n)
            pltpu.make_async_remote_copy(
                src_ref=recv.at[origin],
                dst_ref=recv.at[origin],
                send_sem=send_sem.at[step, c, k],
                recv_sem=recv_sem.at[step, c, k],
                device_id=(origin, near) if step % 4 == 0 else (far, origin),
                device_id_type=pl.DeviceIdType.MESH,
            ).wait_recv()

    def put(which, matrix):
        w_ref[which, 0], w_ref[which, 1] = parts(matrix)

    def get(which, rows, columns):
        return w_ref[which, 0, rows, columns], w_ref[which, 1, rows, columns]

    every = slice(None)

    def half(c):
        return slice(c * order, (c + 1) * order)

    def tops(x):
        pieces = []
        for c in range(2):
            for h in range(high):
                pieces.append(
                    jnp.concatenate(
                        [
                            x[(c * rest + t) * upper : (c * rest + t + 1) * upper, h * lows : (h + 1) * lows]
                            for t in range(rest)
                        ],
                        axis=1,
                    )
                )
        return jnp.concatenate(pieces, axis=0)

    for c in range(2):
        launch(0, c)
    for load in loads:
        load.wait()
    for step in range(sections):
        rnd, section = step // 4, step % 4
        recv = recvs[step]
        low = complex_matrix(gr_ref[rnd, section, 0], gi_ref[rnd, section, 0])
        put(0, low.T if section in (0, 3) else low)
        put(
            1,
            complex_matrix(
                jnp.concatenate(
                    [gr_ref[rnd, section, 1, pl.ds(t, upper, stride=rest), :] for t in range(rest)], axis=0
                ),
                jnp.concatenate(
                    [gi_ref[rnd, section, 1, pl.ds(t, upper, stride=rest), :] for t in range(rest)], axis=0
                ),
            ),
        )
        put(2, complex_matrix(gr_ref[rnd, section, 2], gi_ref[rnd, section, 2]))
        begun = []
        for c in range(2):
            arrive(step, c)
            if section in (1, 2):
                tall = jnp.concatenate([recv[c, :, h].reshape(order, -1) for h in range(high)], axis=1)
                begun.append(dot(get(2 - section, every, half(c)), parts(tall), ((1,), (0,))))
            else:
                wide = recv[c].reshape(high * order, lows)
                begun.append(dot(parts(wide), get(0, half(c), every), ((1,), (0,))))
        state = begun[0] + begun[1]
        if section != 1:
            wide = state.T if section == 2 else state
            tall = jnp.concatenate(
                [
                    jnp.concatenate(
                        [wide[h * order : (h + 1) * order, c * lows : (c + 1) * lows] for h in range(high)], axis=1
                    )
                    for c in range(2)
                ],
                axis=0,
            )
            state = dot(get(1, every, every), parts(tall), ((1,), (0,)))
        ready = parts(tops(state))
        for c in range(2):
            out = dot(get(2, half(c), every), ready, ((1,), (0,)))
            for h in range(high):
                for t in range(rest):
                    part = out[h * upper : (h + 1) * upper, t * lows : (t + 1) * lows]
                    if section == 1:
                        x_ref[c, h, pl.ds(t, upper, stride=rest), :] = part
                    elif step == sections - 1:
                        (or_ref, oi_ref)[c][h, pl.ds(t, upper, stride=rest), :] = part
                    elif section == 0:
                        count = upper // nnear
                        for b in range(nnear):
                            sends[step][c, b, h, pl.ds(t, count, stride=rest), :] = part[
                                b * count : (b + 1) * count
                            ]
                    else:
                        n = nnear if section == 2 else nfar
                        count = high * upper // n
                        for i in range(n // high):
                            sends[step][c, h * (n // high) + i, pl.ds(t, count, stride=rest), :] = part[
                                i * count : (i + 1) * count
                            ]
            if section != 1 and step < sections - 1:
                launch(step + 1, c)
        if section == 1:
            wide = parts(jnp.concatenate([x_ref[c].reshape(high * order, lows) for c in range(2)], axis=1))
            count = lows // nnear
            for c in range(2):
                turned = dot(get(0, half(c), every), wide, ((1,), (1,)))
                for h in range(high):
                    for b in range(nnear):
                        sends[step][c, b, h] = turned[b * count : (b + 1) * count, h * order : (h + 1) * order]
                launch(step + 1, c)
    for copy in pending:
        copy.wait_send()


def one_kernel(nfar, nnear, state_real, state_imag, gate_real, gate_imag):
    shape = state_real.shape
    high, order, lows = shape[2:]
    rounds = gate_real.shape[0]
    sections = 4 * rounds
    kinds = (
        (2, nfar, high * order // nfar, lows),
        (2, nnear, high, order // nnear, lows),
        (2, nnear, high, lows // nnear, order),
        (2, nnear, high * order // nnear, lows),
    )
    buffers = [pltpu.VMEM(kinds[step % 4], jnp.float32) for step in range(sections)]
    most = max(nfar, nnear)
    vmem = pl.BlockSpec(memory_space=pltpu.VMEM)
    anywhere = pl.BlockSpec(memory_space=pl.ANY)
    result = pltpu.VMEM((high, order, lows), jnp.float32)
    real, imag = pl.pallas_call(
        functools.partial(kernel, (nfar, nnear, rounds, high, order, lows)),
        out_shape=(result, result),
        in_specs=[vmem, vmem, anywhere, anywhere],
        out_specs=(vmem, vmem),
        scratch_shapes=buffers[1:]
        + buffers
        + [
            pltpu.VMEM(gate_real.shape, jnp.float32),
            pltpu.VMEM(gate_imag.shape, jnp.float32),
            pltpu.VMEM((3, 2, 2 * order, 2 * order), jnp.bfloat16),
            pltpu.VMEM((2, high, order, lows), jnp.float32),
            pltpu.SemaphoreType.DMA((sections, 2, most)),
            pltpu.SemaphoreType.DMA((sections, 2, most)),
            pltpu.SemaphoreType.DMA((sections, 2)),
            pltpu.SemaphoreType.DMA((2,)),
        ],
        compiler_params=pltpu.CompilerParams(collective_id=0, has_side_effects=True),
    )(
        state_real.reshape(kinds[0][1:]),
        state_imag.reshape(kinds[0][1:]),
        gate_real,
        gate_imag,
    )
    return real.reshape(shape), imag.reshape(shape)


def solution(mesh):
    nfar, nnear = mesh.shape["far"], mesh.shape["near"]

    def body(state_real, state_imag, gate_real, gate_imag):
        high, order, lows = state_real.shape[2:]
        tiles = (high * order // nfar, order // high // nnear, lows // nnear, high * order // nnear)
        if any(rows < 8 or rows % 8 for rows in tiles):
            return on_device(state_real, state_imag, gate_real, gate_imag)
        return one_kernel(nfar, nnear, state_real, state_imag, gate_real, gate_imag)

    return jax.shard_map(
        body,
        mesh=mesh,
        in_specs=(P("far", "near", None, None, None), P("far", "near", None, None, None), P(), P()),
        out_specs=(P("far", "near", None, None, None), P("far", "near", None, None, None)),
        check_vma=False,
    )
```

profile of v0, /device:TPU:0, one launch (start us, length us, event | category | flops | bytes accessed | tf_op | source)
XLA Modules:
  0.0 60.3 jit_solution(14168383639090815981)
XLA Ops:
  0.6 58.3 %shard_map.59 = (f32[2,128,128]{2,1,0:T(8,128)S(1)}, f32[2,128,128]{2,1,0:T(8,128)S(1)}) custom-call(f32[4,64,128]{2,1,0:T(8,128)} %bitcast.6, f32[4,64,128]{2,1,0:T(8,128)} %bitcast.7, f32[2,4,3,128,128]{4,3,2,1,0:T(8,128)} %gr_hbm.1, f32[2,4,3,128,128]{4,3,2,1,0:T(8,128)} %gi_hbm.1), custom_call_target="tpu_custom_call" | custom-call | tf_op jit(solution)/shard_map/pallas_call | solution.py:308
  58.9 0.7 %copy.8 = f32[1,1,2,128,128]{4,3,2,1,0:T(8,128)} copy(f32[1,1,2,128,128]{4,3,2,1,0:T(8,128)S(1)} %bitcast.5) | data formatting | bytes 262144
  59.6 0.7 %copy.9 = f32[1,1,2,128,128]{4,3,2,1,0:T(8,128)} copy(f32[1,1,2,128,128]{4,3,2,1,0:T(8,128)S(1)} %bitcast.4) | data formatting | bytes 262144
where the time goes:
time: 60.4 us; the launch traced here: 60.3 us
  Pallas kernels  58.3 us (97%)
  local copies, waits for them, and re-layouts  1.31 us (2%)
  between operations  0.64 us (1%)
    pallas_call x1, Pallas kernels, one_kernel(): pl.pallas_call(functools.partial(kernel, (nfar, nnear, rounds, high, orde...  58.3 us
    unnamed x2, local copies, waits for them, and re-layouts  1.31 us

commit v1 on v0

v1 whole, which is shorter than its diff:
```python
import functools

import jax
import jax.numpy as jnp
from jax import lax
from jax.experimental import pallas as pl
from jax.experimental.pallas import tpu as pltpu
from jax.sharding import PartitionSpec as P


def gate_low(x, g):
    return jnp.einsum(
        "...l,jl->...j", x, g, precision=lax.Precision.HIGHEST, preferred_element_type=jnp.float32
    )


def gate_mid(x, g):
    return jnp.einsum(
        "...ml,jm->...jl", x, g, precision=lax.Precision.HIGHEST, preferred_element_type=jnp.float32
    )


def gate_top(x, g):
    high, width, lows = (x.shape[-3], x.shape[-2], x.shape[-1])
    upper = g.shape[0] // high
    lead = x.shape[:-3]
    viewed = x.reshape(lead + (high, upper, width // upper, lows))
    matrix = g.reshape((g.shape[0], high, upper))
    out = jnp.einsum(
        "...hkrl,jhk->...jrl",
        viewed,
        matrix,
        precision=lax.Precision.HIGHEST,
        preferred_element_type=jnp.float32,
    )
    return out.reshape(lead + (high, width, lows))


def complex_gate(form, real, imag, greal, gimag):
    new_real = form(real, greal) - form(imag, gimag)
    new_imag = form(imag, greal) + form(real, gimag)
    return (new_real, new_imag)


def merged_rows(x):
    return x.reshape((1, 1, x.shape[2] * x.shape[3], x.shape[4]))


def on_device(state_real, state_imag, gate_real, gate_imag):
    real, imag = (state_real, state_imag)
    forms = (gate_low, gate_mid, gate_top)
    shape = state_real.shape
    for rnd in range(gate_real.shape[0]):
        for section in range(4):
            if section == 2:
                order = [1, 0, 2]
            else:
                order = [0, 1, 2]
            early = []
            later = order[len(early) :]
            pair = (real, imag)
            if section == 0:
                moved = (
                    lax.all_to_all(
                        merged_rows(pair[0]), "far", split_axis=2, concat_axis=2, tiled=True
                    ),
                    lax.all_to_all(
                        merged_rows(pair[1]), "far", split_axis=2, concat_axis=2, tiled=True
                    ),
                )
                pair = (moved[0].reshape(shape), moved[1].reshape(shape))
            elif section == 1:
                pair = (
                    lax.all_to_all(pair[0], "near", split_axis=3, concat_axis=3, tiled=True),
                    lax.all_to_all(pair[1], "near", split_axis=3, concat_axis=3, tiled=True),
                )
            elif section == 2:
                pair = (
                    lax.all_to_all(pair[0], "near", split_axis=4, concat_axis=4, tiled=True),
                    lax.all_to_all(pair[1], "near", split_axis=4, concat_axis=4, tiled=True),
                )
            else:
                moved = (
                    lax.all_to_all(
                        merged_rows(pair[0]), "near", split_axis=2, concat_axis=2, tiled=True
                    ),
                    lax.all_to_all(
                        merged_rows(pair[1]), "near", split_axis=2, concat_axis=2, tiled=True
                    ),
                )
                pair = (moved[0].reshape(shape), moved[1].reshape(shape))
            for which in later:
                pair = complex_gate(
                    forms[which],
                    pair[0],
                    pair[1],
                    gate_real[rnd, section, which],
                    gate_imag[rnd, section, which],
                )
            real, imag = pair
    return (real, imag)


def parts(x):
    first = x.astype(jnp.bfloat16)
    return first, (x - first.astype(jnp.float32)).astype(jnp.bfloat16)


def dot(a, b, dims=((1,), (0,))):
    def product(x, y):
        return lax.dot_general(x, y, (dims, ((), ())), preferred_element_type=jnp.float32)

    return product(a[0], b[0]) + (product(a[0], b[1]) + product(a[1], b[0]))


def product(a, b):
    n = a[0].shape[0]
    w = b[0].shape[1]
    out = dot(parts(jnp.concatenate(a, axis=0)), parts(jnp.concatenate(b, axis=1)))
    return out[:n, :w] - out[n:, w:], out[n:, :w] + out[:n, w:]


def trade(x, row, lane, count):
    rows, lanes = x.shape
    at = lax.broadcasted_iota(jnp.int32, (row, lanes), 1)
    for _ in range(count):
        low = lax.rem(lax.div(at, lane), 2) == 0
        pieces = []
        for start in range(0, rows, 2 * row):
            a, b = x[start : start + row], x[start + row : start + 2 * row]
            pieces.append(jnp.where(low, a, pltpu.roll(b, lane, 1)))
            pieces.append(jnp.where(low, pltpu.roll(a, lanes - lane, 1), b))
        x = jnp.concatenate(pieces, axis=0)
        row, lane, at = row // 2, lane // 2, at[: row // 2]
    return x


def kernel(sizes, sr_hbm, si_hbm, gr_hbm, gi_hbm, or_ref, oi_ref, *scratch):
    nfar, nnear, high, order, lows = sizes
    (
        st_ref, gr_ref, gi_ref, kf_ref, km_ref, w_ref,
        send0, send1, send2, send3, recv0, recv1, recv2, recv3,
        send_sem, recv_sem, load_sem,
    ) = scratch
    sends, recvs = (send0, send1, send2, send3), (recv0, recv1, recv2, recv3)
    far, near = lax.axis_index("far"), lax.axis_index("near")
    upper = order // high
    rest = order // upper
    rows = high * order
    chunks = 2
    fine = lows // chunks // nnear
    half = lows // chunks

    barrier = pltpu.get_barrier_semaphore()
    for k in range(1, nfar):
        pl.semaphore_signal(
            barrier, inc=1, device_id=(lax.rem(far + k, nfar), near), device_id_type=pl.DeviceIdType.MESH
        )
    for k in range(1, nnear):
        pl.semaphore_signal(
            barrier, inc=1, device_id=(far, lax.rem(near + k, nnear)), device_id_type=pl.DeviceIdType.MESH
        )
    first = [
        pltpu.make_async_copy(gr_hbm.at[0, pl.ds(0, 2), 0], gr_ref.at[0, pl.ds(0, 2), 0], load_sem.at[0]),
        pltpu.make_async_copy(gi_hbm.at[0, pl.ds(0, 2), 0], gi_ref.at[0, pl.ds(0, 2), 0], load_sem.at[1]),
        pltpu.make_async_copy(sr_hbm, st_ref.at[0], load_sem.at[2]),
        pltpu.make_async_copy(si_hbm, st_ref.at[1], load_sem.at[3]),
    ]
    others = []
    at = 4
    for rnd in range(2):
        for hbm, ref in ((gr_hbm, gr_ref), (gi_hbm, gi_ref)):
            pieces = [(pl.ds(0, 4), pl.ds(1, 2))]
            pieces += [(pl.ds(2, 2), pl.ds(0, 1))] if rnd == 0 else [(pl.ds(0, 4), pl.ds(0, 1))]
            for s, g in pieces:
                others.append(pltpu.make_async_copy(hbm.at[rnd, s, g], ref.at[rnd, s, g], load_sem.at[at]))
                at += 1
    for load in first + others:
        load.start()

    pending = []

    def launch(stage, c):
        n, me = (nfar, far) if stage % 2 == 0 else (nnear, near)
        source, target = sends[stage].at[c], recvs[stage].at[c]
        for k in ([2, 3, 1] if n == 4 else [6, 7, 5, 2, 3, 4, 1] if n == 8 else range(1, n)):
            to = lax.rem(me + k, n)
            copy = pltpu.make_async_remote_copy(
                src_ref=source.at[to],
                dst_ref=target.at[me],
                send_sem=send_sem.at[stage, c, k],
                recv_sem=recv_sem.at[stage, c, k],
                device_id=(to, near) if stage % 2 == 0 else (far, to),
                device_id_type=pl.DeviceIdType.MESH,
            )
            copy.start()
            pending.append(copy)
        target[me] = source[me]

    def arrive(stage, c):
        n, me = (nfar, far) if stage % 2 == 0 else (nnear, near)
        target = recvs[stage].at[c]
        for k in range(1, n):
            origin = lax.rem(me + n - k, n)
            pltpu.make_async_remote_copy(
                src_ref=target.at[origin],
                dst_ref=target.at[origin],
                send_sem=send_sem.at[stage, c, k],
                recv_sem=recv_sem.at[stage, c, k],
                device_id=(origin, near) if stage % 2 == 0 else (far, origin),
                device_id_type=pl.DeviceIdType.MESH,
            ).wait_recv()

    def gate(s, which):
        return gr_ref[s // 4, s % 4, which], gi_ref[s // 4, s % 4, which]

    def finer(x):
        return jnp.concatenate(
            [
                x[(b * chunks + c) * fine : (b * chunks + c + 1) * fine]
                for c in range(chunks)
                for b in range(nnear)
            ],
            axis=0,
        )

    def split_rows(re, im):
        re, im = finer(re), finer(im)
        left, right = [], []
        for c in range(chunks):
            piece = slice(c * half, (c + 1) * half)
            left += [re[piece], im[piece]]
            right += [-im[piece], re[piece]]
        return jnp.concatenate([jnp.concatenate(left, axis=0), jnp.concatenate(right, axis=0)], axis=1)

    def chunked_columns(x):
        return jnp.concatenate([finer(x[:lows])[:half], finer(x[lows:])[:half],
                                finer(x[:lows])[half:], finer(x[lows:])[half:]], axis=0)

    def put_low(at, re, im, finely):
        if finely:
            wide = split_rows(re, im)
        else:
            wide = jnp.concatenate(
                [jnp.concatenate([re, im], axis=0), jnp.concatenate([-im, re], axis=0)], axis=1
            )
        w_ref[at, 0], w_ref[at, 1] = parts(chunked_columns(wide.T))

    def tops_after_mids(s):
        tr, ti = gate(s, 2)
        left = parts(
            jnp.concatenate(
                [jnp.concatenate([tr, -ti], axis=1), jnp.concatenate([ti, tr], axis=1)], axis=0
            )
        )
        zero = jnp.zeros((upper, order), jnp.float32)
        for t in range(rest):
            blocks = []
            for ref in (gr_ref, gi_ref):
                mid = ref[s // 4, s % 4, 1, pl.ds(t, upper, stride=rest), :]
                for h in range(high):
                    blocks.append(jnp.concatenate([mid if g == h else zero for g in range(high)], axis=1))
            out = dot(left, parts(jnp.concatenate(blocks, axis=0)))
            for c in range(2):
                for h in range(high):
                    for g in range(high):
                        kf_ref[c, g, h, pl.ds(t, upper, stride=rest), :] = out[
                            c * order + h * upper : c * order + (h + 1) * upper, g * order : (g + 1) * order
                        ]
        return tuple(
            jnp.concatenate([kf_ref[c, g].reshape(rows, order) for g in range(high)], axis=1) for c in range(2)
        )

    def put_high(at, pair):
        km_ref[at, 0], km_ref[at, 1] = parts(jnp.concatenate(pair, axis=0))

    def high_of(at):
        return km_ref[at, 0], km_ref[at, 1]

    lane = lax.broadcasted_iota(jnp.int32, (rows, lows), 1)
    sign = jnp.where(lane < half, -1.0, 1.0)

    def apply(at, x):
        out = dot(high_of(at), parts(x))
        return out[:rows] + sign * pltpu.roll(out[rows:], half, 1)

    first[0].wait()
    first[1].wait()
    l1, l0 = gate(1, 0), gate(0, 0)
    low = parts(split_rows(*product(l1, l0)))
    first[2].wait()
    first[3].wait()
    state = jnp.concatenate([st_ref[0], st_ref[1]], axis=1)
    state = dot(parts(state), low, ((1,), (1,)))
    for c in range(chunks):
        sends[0][c] = state[:, c * lows : (c + 1) * lows].reshape(nfar, rows // nfar, lows)
    pl.semaphore_wait(barrier, nfar - 1 + nnear - 1)
    for c in range(chunks):
        launch(0, c)

    for load in others:
        load.wait()
    put_high(0, tops_after_mids(0))
    put_high(1, tops_after_mids(2))
    k1 = tops_after_mids(1)
    out = dot(high_of(1), parts(jnp.concatenate(k1, axis=1)))
    put_high(1, (out[:rows, :rows] - out[rows:, rows:], out[rows:, :rows] + out[:rows, rows:]))
    put_high(2, tops_after_mids(3))

    count = order // nnear
    for c in range(chunks):
        arrive(0, c)
        x = apply(0, recvs[0][c].reshape(rows, lows))
        for b in range(nnear):
            for h in range(high):
                sends[1][c, b, h] = x[h * order + b * count : h * order + (b + 1) * count]
        launch(1, c)
        if c == 0:
            put_high(3, tops_after_mids(4))

    for c in range(chunks):
        arrive(1, c)
        x = jnp.concatenate([recvs[1][c, :, h].reshape(order, lows) for h in range(high)], axis=0)
        x = trade(apply(1, x), rows // 2, half // 2, 3)
        sends[2][c] = apply(2, x).reshape(nfar, rows // nfar, lows)
        launch(2, c)

    put_high(4, tops_after_mids(6))
    k5 = tops_after_mids(5)
    out = dot(high_of(4), parts(jnp.concatenate(k5, axis=1)))
    put_high(4, (out[:rows, :rows] - out[rows:, rows:], out[rows:, :rows] + out[:rows, rows:]))
    put_low(0, *product(gate(5, 0), product(gate(4, 0), product(gate(3, 0), gate(2, 0)))), True)

    for c in range(chunks):
        arrive(2, c)
        x = apply(3, recvs[2][c].reshape(rows, lows))
        x = trade(x, rows // 4, half // 2, 3)
        sends[3][c] = apply(4, x).reshape(nnear, rows // nnear, lows)
        launch(3, c)

    put_high(5, tops_after_mids(7))
    put_low(1, *product(gate(7, 0), gate(6, 0)), False)

    begun = []
    for c in range(chunks):
        arrive(3, c)
        x = trade(recvs[3][c].reshape(rows, lows), rows // 2, half // 2, 3)
        piece = slice(c * lows, (c + 1) * lows)
        begun.append(dot(parts(x), (w_ref[0, 0, piece], w_ref[0, 1, piece])))
    x = begun[0] + begun[1]
    x = jnp.concatenate([trade(x[:, c * lows : (c + 1) * lows], rows // 2, half // 2, 3) for c in range(chunks)], axis=1)
    x = dot(parts(x), (w_ref[1, 0], w_ref[1, 1]))
    out = dot(high_of(5), parts(x))
    or_ref[...] = out[:rows, :lows] - out[rows:, lows:]
    oi_ref[...] = out[rows:, :lows] + out[:rows, lows:]
    for copy in pending:
        copy.wait_send()


def one_kernel(nfar, nnear, state_real, state_imag, gate_real, gate_imag):
    shape = state_real.shape
    high, order, lows = shape[2:]
    rows = high * order
    blocks = (
        (2, nfar, rows // nfar, lows),
        (2, nnear, high, order // nnear, lows),
        (2, nfar, rows // nfar, lows),
        (2, nnear, rows // nnear, lows),
    )
    buffers = [pltpu.VMEM(block, jnp.float32) for block in blocks]
    vmem = pl.BlockSpec(memory_space=pltpu.VMEM)
    anywhere = pl.BlockSpec(memory_space=pl.ANY)
    result = pltpu.VMEM((rows, lows), jnp.float32)
    real, imag = pl.pallas_call(
        functools.partial(kernel, (nfar, nnear, high, order, lows)),
        out_shape=(result, result),
        in_specs=[anywhere] * 4,
        out_specs=(vmem, vmem),
        scratch_shapes=[
            pltpu.VMEM((2, rows, lows), jnp.float32),
            pltpu.VMEM(gate_real.shape, jnp.float32),
            pltpu.VMEM(gate_imag.shape, jnp.float32),
            pltpu.VMEM((2, high, high, order, order), jnp.float32),
            pltpu.VMEM((6, 2, 2 * rows, rows), jnp.bfloat16),
            pltpu.VMEM((2, 2, 2 * lows, 2 * lows), jnp.bfloat16),
        ]
        + buffers
        + buffers
        + [
            pltpu.SemaphoreType.DMA((4, 2, max(nfar, nnear))),
            pltpu.SemaphoreType.DMA((4, 2, max(nfar, nnear))),
            pltpu.SemaphoreType.DMA((12,)),
        ],
        compiler_params=pltpu.CompilerParams(collective_id=0, has_side_effects=True),
    )(
        state_real.reshape(rows, lows),
        state_imag.reshape(rows, lows),
        gate_real,
        gate_imag,
    )
    return real.reshape(shape), imag.reshape(shape)


def solution(mesh):
    nfar, nnear = mesh.shape["far"], mesh.shape["near"]

    def body(state_real, state_imag, gate_real, gate_imag):
        high, order, lows = state_real.shape[2:]
        fits = nfar == high * high and nnear == high * nfar and order == lows and gate_real.shape[0] == 2
        fits = fits and high == 2 and lows // nnear // 2 == 8
        if not fits:
            return on_device(state_real, state_imag, gate_real, gate_imag)
        return one_kernel(nfar, nnear, state_real, state_imag, gate_real, gate_imag)

    return jax.shard_map(
        body,
        mesh=mesh,
        in_specs=(P("far", "near", None, None, None), P("far", "near", None, None, None), P(), P()),
        out_specs=(P("far", "near", None, None, None), P("far", "near", None, None, None)),
        check_vma=False,
    )
```

time: 60.4 us -> 34.2 us (0.57)
  Pallas kernels: 58.3 us -> 32.1 us
    pallas_call x1, Pallas kernels: 58.3 us -> 32.1 us  [one_kernel(): pl.pallas_call(functools.partial(kernel, (nfar, nnear, high, order, lows)...]
where the time goes in v1:
time: 34.2 us; the launch traced here: 34 us
  Pallas kernels  32.1 us (94%)
  local copies, waits for them, and re-layouts  1.31 us (4%)
  between operations  0.64 us (2%)
    pallas_call x1, Pallas kernels, one_kernel(): pl.pallas_call(functools.partial(kernel, (nfar, nnear, high, order, lows)...  32.1 us
    unnamed x2, local copies, waits for them, and re-layouts  1.31 us

profile of v1, /device:TPU:0, one launch (start us, length us, event | category | flops | bytes accessed | tf_op | source)
XLA Modules:
  0.0 34.0 jit_solution(9973896644953580572)
XLA Ops:
  0.6 32.1 %shard_map.59 = (f32[256,128]{1,0:T(8,128)S(1)}, f32[256,128]{1,0:T(8,128)S(1)}) custom-call(f32[256,128]{1,0:T(8,128)} %bitcast.6, f32[256,128]{1,0:T(8,128)} %bitcast.7, f32[2,4,3,128,128]{4,3,2,1,0:T(8,128)} %gr_hbm.1, f32[2,4,3,128,128]{4,3,2,1,0:T(8,128)} %gi_hbm.1), custom_call_target="tpu_custom_call" | custom-call | tf_op jit(solution)/shard_map/pallas_call | solution.py:374
  32.7 0.7 %copy.8 = f32[1,1,2,128,128]{4,3,2,1,0:T(8,128)} copy(f32[1,1,2,128,128]{4,3,2,1,0:T(8,128)S(1)} %bitcast.5) | data formatting | bytes 262144
  33.4 0.7 %copy.9 = f32[1,1,2,128,128]{4,3,2,1,0:T(8,128)} copy(f32[1,1,2,128,128]{4,3,2,1,0:T(8,128)S(1)} %bitcast.4) | data formatting | bytes 262144

commit v2 on v1

--- a/solution.py
+++ b/solution.py
@@ -138,7 +138,7 @@
 def kernel(sizes, sr_hbm, si_hbm, gr_hbm, gi_hbm, or_ref, oi_ref, *scratch):
     nfar, nnear, high, order, lows = sizes
     (
-        st_ref, gr_ref, gi_ref, kf_ref, km_ref, w_ref,
+        st_ref, lr_ref, li_ref, gr_ref, gi_ref, kf_ref, km_ref, w_ref,
         send0, send1, send2, send3, recv0, recv1, recv2, recv3,
         send_sem, recv_sem, load_sem,
     ) = scratch
@@ -161,24 +161,17 @@
             barrier, inc=1, device_id=(far, lax.rem(near + k, nnear)), device_id_type=pl.DeviceIdType.MESH
         )
     first = [
-        pltpu.make_async_copy(gr_hbm.at[0, pl.ds(0, 2), 0], gr_ref.at[0, pl.ds(0, 2), 0], load_sem.at[0]),
-        pltpu.make_async_copy(gi_hbm.at[0, pl.ds(0, 2), 0], gi_ref.at[0, pl.ds(0, 2), 0], load_sem.at[1]),
+        pltpu.make_async_copy(gr_hbm.at[0, pl.ds(0, 2), 0], lr_ref, load_sem.at[0]),
+        pltpu.make_async_copy(gi_hbm.at[0, pl.ds(0, 2), 0], li_ref, load_sem.at[1]),
         pltpu.make_async_copy(sr_hbm, st_ref.at[0], load_sem.at[2]),
         pltpu.make_async_copy(si_hbm, st_ref.at[1], load_sem.at[3]),
     ]
-    others = []
-    at = 4
-    for rnd in range(2):
-        for hbm, ref in ((gr_hbm, gr_ref), (gi_hbm, gi_ref)):
-            pieces = [(pl.ds(0, 4), pl.ds(1, 2))]
-            pieces += [(pl.ds(2, 2), pl.ds(0, 1))] if rnd == 0 else [(pl.ds(0, 4), pl.ds(0, 1))]
-            for s, g in pieces:
-                others.append(pltpu.make_async_copy(hbm.at[rnd, s, g], ref.at[rnd, s, g], load_sem.at[at]))
-                at += 1
+    others = [
+        pltpu.make_async_copy(gr_hbm, gr_ref, load_sem.at[4]),
+        pltpu.make_async_copy(gi_hbm, gi_ref, load_sem.at[5]),
+    ]
     for load in first + others:
         load.start()
-
-    pending = []
 
     def launch(stage, c):
         n, me = (nfar, far) if stage % 2 == 0 else (nnear, near)
@@ -188,28 +181,18 @@
             copy = pltpu.make_async_remote_copy(
                 src_ref=source.at[to],
                 dst_ref=target.at[me],
-                send_sem=send_sem.at[stage, c, k],
-                recv_sem=recv_sem.at[stage, c, k],
+                send_sem=send_sem.at[stage],
+                recv_sem=recv_sem.at[stage, c],
                 device_id=(to, near) if stage % 2 == 0 else (far, to),
                 device_id_type=pl.DeviceIdType.MESH,
             )
             copy.start()
-            pending.append(copy)
         target[me] = source[me]
 
     def arrive(stage, c):
-        n, me = (nfar, far) if stage % 2 == 0 else (nnear, near)
-        target = recvs[stage].at[c]
-        for k in range(1, n):
-            origin = lax.rem(me + n - k, n)
-            pltpu.make_async_remote_copy(
-                src_ref=target.at[origin],
-                dst_ref=target.at[origin],
-                send_sem=send_sem.at[stage, c, k],
-                recv_sem=recv_sem.at[stage, c, k],
-                device_id=(origin, near) if stage % 2 == 0 else (far, origin),
-                device_id_type=pl.DeviceIdType.MESH,
-            ).wait_recv()
+        n = nfar if stage % 2 == 0 else nnear
+        landed = recvs[stage].at[c, pl.ds(0, n - 1)]
+        pltpu.make_async_copy(landed, landed, recv_sem.at[stage, c]).wait()
 
     def gate(s, which):
         return gr_ref[s // 4, s % 4, which], gi_ref[s // 4, s % 4, which]
@@ -286,8 +269,7 @@
 
     first[0].wait()
     first[1].wait()
-    l1, l0 = gate(1, 0), gate(0, 0)
-    low = parts(split_rows(*product(l1, l0)))
+    low = parts(split_rows(*product((lr_ref[1], li_ref[1]), (lr_ref[0], li_ref[0]))))
     first[2].wait()
     first[3].wait()
     state = jnp.concatenate([st_ref[0], st_ref[1]], axis=1)
@@ -353,8 +335,9 @@
     out = dot(high_of(5), parts(x))
     or_ref[...] = out[:rows, :lows] - out[rows:, lows:]
     oi_ref[...] = out[rows:, :lows] + out[:rows, lows:]
-    for copy in pending:
-        copy.wait_send()
+    for stage in range(4):
+        sent = sends[stage].at[:, pl.ds(0, (nfar if stage % 2 == 0 else nnear) - 1)]
+        pltpu.make_async_copy(sent, sent, send_sem.at[stage]).wait()
 
 
 def one_kernel(nfar, nnear, state_real, state_imag, gate_real, gate_imag):
@@ -378,6 +361,8 @@
         out_specs=(vmem, vmem),
         scratch_shapes=[
             pltpu.VMEM((2, rows, lows), jnp.float32),
+            pltpu.VMEM((2, order, order), jnp.float32),
+            pltpu.VMEM((2, order, order), jnp.float32),
             pltpu.VMEM(gate_real.shape, jnp.float32),
             pltpu.VMEM(gate_imag.shape, jnp.float32),
             pltpu.VMEM((2, high, high, order, order), jnp.float32),
@@ -387,9 +372,9 @@
         + buffers
         + buffers
         + [
-            pltpu.SemaphoreType.DMA((4, 2, max(nfar, nnear))),
-            pltpu.SemaphoreType.DMA((4, 2, max(nfar, nnear))),
-            pltpu.SemaphoreType.DMA((12,)),
+            pltpu.SemaphoreType.DMA((4,)),
+            pltpu.SemaphoreType.DMA((4, 2)),
+            pltpu.SemaphoreType.DMA((6,)),
         ],
         compiler_params=pltpu.CompilerParams(collective_id=0, has_side_effects=True),
     )(

time: 34.2 us -> 33 us (0.965)
  Pallas kernels: 32.1 us -> 30.9 us
    pallas_call x1, Pallas kernels: 32.1 us -> 30.9 us  [one_kernel(): pl.pallas_call(functools.partial(kernel, (nfar, nnear, high, order, lows)...]
where the time goes in v2:
time: 33 us; the launch traced here: 32.9 us
  Pallas kernels  30.9 us (94%)
  local copies, waits for them, and re-layouts  1.31 us (4%)
  between operations  0.64 us (2%)
    pallas_call x1, Pallas kernels, one_kernel(): pl.pallas_call(functools.partial(kernel, (nfar, nnear, high, order, lows)...  30.9 us
    unnamed x2, local copies, waits for them, and re-layouts  1.31 us

profile of v2, /device:TPU:0, one launch (start us, length us, event | category | flops | bytes accessed | tf_op | source)
XLA Modules:
  0.0 32.9 jit_solution(12232615968880735123)
XLA Ops:
  0.6 30.9 %shard_map.59 = (f32[256,128]{1,0:T(8,128)S(1)}, f32[256,128]{1,0:T(8,128)S(1)}) custom-call(f32[256,128]{1,0:T(8,128)} %bitcast.6, f32[256,128]{1,0:T(8,128)} %bitcast.7, f32[2,4,3,128,128]{4,3,2,1,0:T(8,128)} %gr_hbm.1, f32[2,4,3,128,128]{4,3,2,1,0:T(8,128)} %gi_hbm.1), custom_call_target="tpu_custom_call" | custom-call | tf_op jit(solution)/shard_map/pallas_call | solution.py:357
  31.5 0.7 %copy.8 = f32[1,1,2,128,128]{4,3,2,1,0:T(8,128)} copy(f32[1,1,2,128,128]{4,3,2,1,0:T(8,128)S(1)} %bitcast.5) | data formatting | bytes 262144
  32.2 0.7 %copy.9 = f32[1,1,2,128,128]{4,3,2,1,0:T(8,128)} copy(f32[1,1,2,128,128]{4,3,2,1,0:T(8,128)S(1)} %bitcast.4) | data formatting | bytes 262144

commit v3 on v2

v3 whole, which is shorter than its diff:
```python
import functools

import jax
import jax.numpy as jnp
from jax import lax
from jax.experimental import pallas as pl
from jax.experimental.pallas import tpu as pltpu
from jax.sharding import PartitionSpec as P


def gate_low(x, g):
    return jnp.einsum(
        "...l,jl->...j", x, g, precision=lax.Precision.HIGHEST, preferred_element_type=jnp.float32
    )


def gate_mid(x, g):
    return jnp.einsum(
        "...ml,jm->...jl", x, g, precision=lax.Precision.HIGHEST, preferred_element_type=jnp.float32
    )


def gate_top(x, g):
    high, width, lows = (x.shape[-3], x.shape[-2], x.shape[-1])
    upper = g.shape[0] // high
    lead = x.shape[:-3]
    viewed = x.reshape(lead + (high, upper, width // upper, lows))
    matrix = g.reshape((g.shape[0], high, upper))
    out = jnp.einsum(
        "...hkrl,jhk->...jrl",
        viewed,
        matrix,
        precision=lax.Precision.HIGHEST,
        preferred_element_type=jnp.float32,
    )
    return out.reshape(lead + (high, width, lows))


def complex_gate(form, real, imag, greal, gimag):
    new_real = form(real, greal) - form(imag, gimag)
    new_imag = form(imag, greal) + form(real, gimag)
    return (new_real, new_imag)


def merged_rows(x):
    return x.reshape((1, 1, x.shape[2] * x.shape[3], x.shape[4]))


def on_device(state_real, state_imag, gate_real, gate_imag):
    real, imag = (state_real, state_imag)
    forms = (gate_low, gate_mid, gate_top)
    shape = state_real.shape
    for rnd in range(gate_real.shape[0]):
        for section in range(4):
            if section == 2:
                order = [1, 0, 2]
            else:
                order = [0, 1, 2]
            early = []
            later = order[len(early) :]
            pair = (real, imag)
            if section == 0:
                moved = (
                    lax.all_to_all(
                        merged_rows(pair[0]), "far", split_axis=2, concat_axis=2, tiled=True
                    ),
                    lax.all_to_all(
                        merged_rows(pair[1]), "far", split_axis=2, concat_axis=2, tiled=True
                    ),
                )
                pair = (moved[0].reshape(shape), moved[1].reshape(shape))
            elif section == 1:
                pair = (
                    lax.all_to_all(pair[0], "near", split_axis=3, concat_axis=3, tiled=True),
                    lax.all_to_all(pair[1], "near", split_axis=3, concat_axis=3, tiled=True),
                )
            elif section == 2:
                pair = (
                    lax.all_to_all(pair[0], "near", split_axis=4, concat_axis=4, tiled=True),
                    lax.all_to_all(pair[1], "near", split_axis=4, concat_axis=4, tiled=True),
                )
            else:
                moved = (
                    lax.all_to_all(
                        merged_rows(pair[0]), "near", split_axis=2, concat_axis=2, tiled=True
                    ),
                    lax.all_to_all(
                        merged_rows(pair[1]), "near", split_axis=2, concat_axis=2, tiled=True
                    ),
                )
                pair = (moved[0].reshape(shape), moved[1].reshape(shape))
            for which in later:
                pair = complex_gate(
                    forms[which],
                    pair[0],
                    pair[1],
                    gate_real[rnd, section, which],
                    gate_imag[rnd, section, which],
                )
            real, imag = pair
    return (real, imag)


def parts(x):
    first = x.astype(jnp.bfloat16)
    return first, (x - first.astype(jnp.float32)).astype(jnp.bfloat16)


def dot(a, b, dims=((1,), (0,))):
    def product(x, y):
        return lax.dot_general(x, y, (dims, ((), ())), preferred_element_type=jnp.float32)

    return product(a[0], b[0]) + (product(a[0], b[1]) + product(a[1], b[0]))


def complex_rows(stacked, pair):
    out = dot(stacked, parts(jnp.concatenate(pair, axis=1)))
    n, w = out.shape[0] // 2, out.shape[1] // 2
    return out[:n, :w] - out[n:, w:], out[n:, :w] + out[:n, w:]


def product(a, b):
    return complex_rows(parts(jnp.concatenate(a, axis=0)), b)


def complex_matrix(re, im):
    return jnp.concatenate(
        [jnp.concatenate([re, -im], axis=1), jnp.concatenate([im, re], axis=1)], axis=0
    )


def trade(x, swaps):
    unit = 8
    rows, lanes = x.shape
    at = lax.broadcasted_iota(jnp.int32, (unit, lanes), 1)
    steps = []
    for row, lane in swaps:
        low = lax.rem(lax.div(at, lane), 2) == 0
        steps.append((row // unit, low, jnp.where(low, at + lane, at - lane)))
    out = [None] * (rows // unit)
    for base in range(rows // unit):
        if any(base // stride % 2 for stride, _, _ in steps):
            continue
        group = [base]
        for stride, _, _ in steps:
            group = group + [i + stride for i in group]
        for i in group:
            out[i] = x[i * unit : (i + 1) * unit]
        for stride, low, other in steps:
            for i in group:
                if i // stride % 2 == 0:
                    a, b = out[i], out[i + stride]
                    moved = jnp.take_along_axis(jnp.where(low, b, a), other, axis=1)
                    out[i], out[i + stride] = jnp.where(low, a, moved), jnp.where(low, moved, b)
    return jnp.concatenate(out, axis=0)


def kernel(sizes, sr_hbm, si_hbm, gr_hbm, gi_hbm, or_ref, oi_ref, *scratch):
    nfar, nnear, high, order, lows = sizes
    (
        st_ref, lr_ref, li_ref, gr_ref, gi_ref, kf_ref, km_ref, w_ref,
        send0, send1, send2, recv0, recv1, recv2,
        send_sem, recv_sem, load_sem,
    ) = scratch
    far, near = lax.axis_index("far"), lax.axis_index("near")
    core, side = near % 2, far // 2
    upper = order // high
    rest = order // upper
    rows = high * order
    fine = lows // nnear
    eight = fine // 2

    def flips(at, bits):
        found = []
        for mask in range(2**bits):
            found.append(sum((at // 2**i % 2 + mask // 2**i % 2) % 2 * 2**i for i in range(bits)))
        return found

    fars, nears = flips(far, 2), flips(near, 3)
    others = [(a, b) for a in range(nfar) for b in range(nnear) if a + b]
    others.sort(key=lambda ab: -(ab[0] + ab[1] // 4 + ab[1] // 2 % 2))

    barrier = pltpu.get_barrier_semaphore()
    for a, b in others:
        pl.semaphore_signal(
            barrier, inc=1, device_id=(fars[a], nears[b]), device_id_type=pl.DeviceIdType.MESH
        )
    first = [
        pltpu.make_async_copy(gr_hbm.at[0, pl.ds(0, 2), 0], lr_ref, load_sem.at[0]),
        pltpu.make_async_copy(gi_hbm.at[0, pl.ds(0, 2), 0], li_ref, load_sem.at[1]),
        pltpu.make_async_copy(sr_hbm, st_ref.at[0], load_sem.at[2]),
        pltpu.make_async_copy(si_hbm, st_ref.at[1], load_sem.at[3]),
    ]
    gates = [
        pltpu.make_async_copy(gr_hbm, gr_ref, load_sem.at[4]),
        pltpu.make_async_copy(gi_hbm, gi_ref, load_sem.at[5]),
    ]
    for load in first + gates:
        load.start()

    def remote(stage, source, target, to):
        return pltpu.make_async_remote_copy(
            src_ref=source,
            dst_ref=target,
            send_sem=send_sem.at[stage],
            recv_sem=recv_sem.at[stage],
            device_id=to,
            device_id_type=pl.DeviceIdType.MESH,
        )

    def settle(ref, sem):
        pltpu.make_async_copy(ref, ref, sem).wait()

    def gate(s, which):
        return gr_ref[s // 4, s % 4, which], gi_ref[s // 4, s % 4, which]

    def tops_after_mids(s):
        left = parts(complex_matrix(*gate(s, 2)))
        zero = jnp.zeros((upper, order), jnp.float32)
        for t in range(rest):
            blocks = []
            for ref in (gr_ref, gi_ref):
                mid = ref[s // 4, s % 4, 1, pl.ds(t, upper, stride=rest), :]
                for h in range(high):
                    blocks.append(jnp.concatenate([mid if g == h else zero for g in range(high)], axis=1))
            out = dot(left, parts(jnp.concatenate(blocks, axis=0)))
            for c in range(2):
                for h in range(high):
                    for g in range(high):
                        kf_ref[c, g, h, pl.ds(t, upper, stride=rest), :] = out[
                            c * order + h * upper : c * order + (h + 1) * upper, g * order : (g + 1) * order
                        ]
        return tuple(
            jnp.concatenate([kf_ref[c, g].reshape(rows, order) for g in range(high)], axis=1) for c in range(2)
        )

    def put_high(at, pair):
        km_ref[at, 0], km_ref[at, 1] = parts(jnp.concatenate(pair, axis=0))

    def high_of(at):
        return km_ref[at, 0], km_ref[at, 1]

    def put_low(at, pair, finely):
        wide = complex_matrix(*pair).T
        if finely:
            wide = jnp.concatenate(
                [
                    wide[((c * nnear + b) * 2 + k) * eight : ((c * nnear + b) * 2 + k + 1) * eight]
                    for c in range(2)
                    for k in range(2)
                    for b in range(nnear)
                ],
                axis=0,
            )
        w_ref[at, 0], w_ref[at, 1] = parts(wide)

    def low_gate(at, pair):
        out = dot(parts(jnp.concatenate(pair, axis=1)), (w_ref[at, 0], w_ref[at, 1]))
        return out[:, :lows], out[:, lows:]

    def traded(pair, swaps):
        return tuple(trade(x, swaps) for x in pair)

    first[0].wait()
    first[1].wait()
    last = tuple(
        jnp.concatenate([ref[1, pl.ds(k, nnear, stride=fine), :] for k in range(fine)], axis=0)
        for ref in (lr_ref, li_ref)
    )
    low = parts(complex_matrix(*product(last, (lr_ref[0], li_ref[0]))))
    first[2].wait()
    first[3].wait()
    state = dot(parts(jnp.concatenate([st_ref[0], st_ref[1]], axis=1)), low, ((1,), (1,)))
    pair = traded((state[:, :lows], state[:, lows:]), ((64, 64), (32, 32), (16, 16), (8, 8)))
    for c in range(2):
        for h in range(high):
            for k in range(fine):
                at = (h * fine + k) * eight
                send0[k * high + h, c] = pair[c][at : at + eight]
    pl.semaphore_wait(barrier, nfar * nnear - 1)
    me = far * nnear + near
    for a, b in others:
        remote(0, send0.at[fars[a] * nnear + nears[b]], recv0.at[me], (fars[a], nears[b])).start()
    recv0[me] = send0[me]

    for load in gates:
        load.wait()
    put_high(0, tops_after_mids(0))
    put_high(1, tops_after_mids(2))
    put_high(1, complex_rows(high_of(1), tops_after_mids(1)))
    put_high(2, tops_after_mids(3))
    put_high(3, tops_after_mids(4))
    put_high(4, tops_after_mids(6))
    put_high(4, complex_rows(high_of(4), tops_after_mids(5)))

    settle(recv0.at[pl.ds(0, nfar * nnear - 1)], recv_sem.at[0])
    pair = tuple(recv0[:, c].reshape(rows, lows) for c in range(2))
    pair = complex_rows(high_of(0), traded(pair, ((32, 32), (16, 16), (8, 8))))
    pair = complex_rows(high_of(1), traded(pair, ((64, 32), (32, 16), (16, 8))))
    pair = complex_rows(high_of(2), traded(pair, ((128, 4), (64, 2), (32, 1))))
    for c in range(2):
        for k in range(2):
            send1[k, c] = pair[c][k * order : (k + 1) * order]
    remote(1, send1.at[1 - core], recv1.at[core], (far, nears[1])).start()
    recv1[core] = send1[core]
    settle(recv1.at[0], recv_sem.at[1])

    pair = tuple(recv1[:, c].reshape(rows, lows) for c in range(2))
    pair = complex_rows(high_of(3), traded(pair, ((64, 64),)))
    pair = complex_rows(high_of(4), traded(pair, ((64, 4), (32, 2), (16, 1))))
    pair = traded(pair, ((16, 64),))
    thin = rows // nnear // 2
    for c in range(2):
        for b in range(nnear):
            for k in range(2):
                at = (b * 2 + k) * thin
                send2[k * nnear + b, c] = pair[c][at : at + thin]
    here = far * (nnear // 2) + near // 2
    same = side == core
    for b in (6, 7, 4, 5, 2, 3, 1, 0):
        for a in (1, 0):
            to = (core * 2 + (far % 2 + a) % 2, nears[b])
            copy = remote(2, send2.at[to[0] % 2 * nnear + to[1]], recv2.at[here], to)
            if a + b:
                copy.start()
            else:
                @pl.when(jnp.logical_not(same))
                def _():
                    copy.start()

                @pl.when(same)
                def _():
                    recv2[here] = send2[far % 2 * nnear + near]

    put_high(5, tops_after_mids(7))
    put_low(0, product(gate(5, 0), product(gate(4, 0), product(gate(3, 0), gate(2, 0)))), True)
    put_low(1, product(gate(7, 0), gate(6, 0)), False)

    count = 2 * nnear

    @pl.when(same)
    def _():
        settle(recv2.at[pl.ds(0, count - 1)], recv_sem.at[2])

    @pl.when(jnp.logical_not(same))
    def _():
        settle(recv2, recv_sem.at[2])

    pair = tuple(recv2[:, c].reshape(rows, lows) for c in range(2))
    pair = low_gate(0, traded(pair, ((128, 64), (64, 4), (32, 2), (16, 1))))
    pair = low_gate(1, traded(pair, ((64, 64), (32, 32), (16, 16))))
    pair = tuple(
        jnp.concatenate(
            [x[(k * nnear + b) * thin : (k * nnear + b + 1) * thin] for b in range(nnear) for k in range(2)], axis=0
        )
        for x in pair
    )
    or_ref[...], oi_ref[...] = complex_rows(high_of(5), pair)

    settle(send0.at[pl.ds(0, nfar * nnear - 1)], send_sem.at[0])
    settle(send1.at[0], send_sem.at[1])

    @pl.when(same)
    def _():
        settle(send2.at[pl.ds(0, count - 1)], send_sem.at[2])

    @pl.when(jnp.logical_not(same))
    def _():
        settle(send2, send_sem.at[2])


def one_kernel(nfar, nnear, state_real, state_imag, gate_real, gate_imag):
    shape = state_real.shape
    high, order, lows = shape[2:]
    rows = high * order
    blocks = (
        (nfar * nnear, 2, rows // nfar // nnear, lows),
        (2, 2, rows // 2, lows),
        (2 * nnear, 2, rows // nnear // 2, lows),
    )
    buffers = [pltpu.VMEM(block, jnp.float32) for block in blocks]
    vmem = pl.BlockSpec(memory_space=pltpu.VMEM)
    anywhere = pl.BlockSpec(memory_space=pl.ANY)
    result = pltpu.VMEM((rows, lows), jnp.float32)
    real, imag = pl.pallas_call(
        functools.partial(kernel, (nfar, nnear, high, order, lows)),
        out_shape=(result, result),
        in_specs=[anywhere] * 4,
        out_specs=(vmem, vmem),
        scratch_shapes=[
            pltpu.VMEM((2, rows, lows), jnp.float32),
            pltpu.VMEM((2, order, order), jnp.float32),
            pltpu.VMEM((2, order, order), jnp.float32),
            pltpu.VMEM(gate_real.shape, jnp.float32),
            pltpu.VMEM(gate_imag.shape, jnp.float32),
            pltpu.VMEM((2, high, high, order, order), jnp.float32),
            pltpu.VMEM((6, 2, 2 * rows, rows), jnp.bfloat16),
            pltpu.VMEM((2, 2, 2 * lows, 2 * lows), jnp.bfloat16),
        ]
        + buffers
        + buffers
        + [
            pltpu.SemaphoreType.DMA((3,)),
            pltpu.SemaphoreType.DMA((3,)),
            pltpu.SemaphoreType.DMA((6,)),
        ],
        compiler_params=pltpu.CompilerParams(collective_id=0, has_side_effects=True),
    )(
        state_real.reshape(rows, lows),
        state_imag.reshape(rows, lows),
        gate_real,
        gate_imag,
    )
    return real.reshape(shape), imag.reshape(shape)


def solution(mesh):
    nfar, nnear = mesh.shape["far"], mesh.shape["near"]

    def body(state_real, state_imag, gate_real, gate_imag):
        high, order, lows = state_real.shape[2:]
        fits = high == 2 and nfar == high**2 and nnear == high**3 and order == lows and gate_real.shape[0] == 2
        fits = fits and lows == 2 * nnear * 8
        if not fits:
            return on_device(state_real, state_imag, gate_real, gate_imag)
        return one_kernel(nfar, nnear, state_real, state_imag, gate_real, gate_imag)

    return jax.shard_map(
        body,
        mesh=mesh,
        in_specs=(P("far", "near", None, None, None), P("far", "near", None, None, None), P(), P()),
        out_specs=(P("far", "near", None, None, None), P("far", "near", None, None, None)),
        check_vma=False,
    )
```

time: 33 us -> 31.2 us (0.945)
  Pallas kernels: 30.9 us -> 29.1 us
    pallas_call x1, Pallas kernels: 30.9 us -> 29.1 us  [one_kernel(): pl.pallas_call(functools.partial(kernel, (nfar, nnear, high, order, lows)...]
where the time goes in v3:
time: 31.2 us; the launch traced here: 31 us
  Pallas kernels  29.1 us (93%)
  local copies, waits for them, and re-layouts  1.31 us (4%)
  between operations  0.64 us (2%)
    pallas_call x1, Pallas kernels, one_kernel(): pl.pallas_call(functools.partial(kernel, (nfar, nnear, high, order, lows)...  29.1 us
    unnamed x2, local copies, waits for them, and re-layouts  1.31 us

profile of v3, /device:TPU:0, one launch (start us, length us, event | category | flops | bytes accessed | tf_op | source)
XLA Modules:
  0.0 31.0 jit_solution(13418803337474109908)
XLA Ops:
  0.6 29.1 %shard_map.59 = (f32[256,128]{1,0:T(8,128)S(1)}, f32[256,128]{1,0:T(8,128)S(1)}) custom-call(f32[256,128]{1,0:T(8,128)} %bitcast.6, f32[256,128]{1,0:T(8,128)} %bitcast.7, f32[2,4,3,128,128]{4,3,2,1,0:T(8,128)} %gr_hbm.1, f32[2,4,3,128,128]{4,3,2,1,0:T(8,128)} %gi_hbm.1), custom_call_target="tpu_custom_call" | custom-call | tf_op jit(solution)/shard_map/pallas_call | solution.py:385
  29.7 0.7 %copy.8 = f32[1,1,2,128,128]{4,3,2,1,0:T(8,128)} copy(f32[1,1,2,128,128]{4,3,2,1,0:T(8,128)S(1)} %bitcast.5) | data formatting | bytes 262144
  30.4 0.7 %copy.9 = f32[1,1,2,128,128]{4,3,2,1,0:T(8,128)} copy(f32[1,1,2,128,128]{4,3,2,1,0:T(8,128)S(1)} %bitcast.4) | data formatting | bytes 262144

commit v4 on v3

--- a/solution.py
+++ b/solution.py
@@ -113,14 +113,18 @@
     return product(a[0], b[0]) + (product(a[0], b[1]) + product(a[1], b[0]))
 
 
+def split(pair):
+    return parts(jnp.concatenate(pair, axis=1))
+
+
 def complex_rows(stacked, pair):
-    out = dot(stacked, parts(jnp.concatenate(pair, axis=1)))
+    out = dot(stacked, pair)
     n, w = out.shape[0] // 2, out.shape[1] // 2
     return out[:n, :w] - out[n:, w:], out[n:, :w] + out[:n, w:]
 
 
 def product(a, b):
-    return complex_rows(parts(jnp.concatenate(a, axis=0)), b)
+    return complex_rows(parts(jnp.concatenate(a, axis=0)), split(b))
 
 
 def complex_matrix(re, im):
@@ -155,12 +159,12 @@
     return jnp.concatenate(out, axis=0)
 
 
-def kernel(sizes, sr_hbm, si_hbm, gr_hbm, gi_hbm, or_ref, oi_ref, *scratch):
+def kernel(sizes, sr_hbm, si_hbm, gr_hbm, gi_hbm, o_ref, *scratch):
     nfar, nnear, high, order, lows = sizes
     (
         st_ref, lr_ref, li_ref, gr_ref, gi_ref, kf_ref, km_ref, w_ref,
         send0, send1, send2, recv0, recv1, recv2,
-        send_sem, recv_sem, load_sem,
+        x_ref, send_sem, recv_sem, load_sem,
     ) = scratch
     far, near = lax.axis_index("far"), lax.axis_index("near")
     core, side = near % 2, far // 2
@@ -198,12 +202,12 @@
     for load in first + gates:
         load.start()
 
-    def remote(stage, source, target, to):
+    def remote(stage, source, target, to, group=0):
         return pltpu.make_async_remote_copy(
             src_ref=source,
             dst_ref=target,
             send_sem=send_sem.at[stage],
-            recv_sem=recv_sem.at[stage],
+            recv_sem=recv_sem.at[stage + group],
             device_id=to,
             device_id_type=pl.DeviceIdType.MESH,
         )
@@ -240,6 +244,10 @@
     def high_of(at):
         return km_ref[at, 0], km_ref[at, 1]
 
+    def rows_of(at, half):
+        places = [pl.ds(pl.multiple_of(half * order, order) + c * rows, order) for c in range(2)]
+        return tuple(jnp.concatenate([km_ref[at, p, place] for place in places], axis=0) for p in range(2))
+
     def put_low(at, pair, finely):
         wide = complex_matrix(*pair).T
         if finely:
@@ -280,57 +288,64 @@
     pl.semaphore_wait(barrier, nfar * nnear - 1)
     me = far * nnear + near
     for a, b in others:
-        remote(0, send0.at[fars[a] * nnear + nears[b]], recv0.at[me], (fars[a], nears[b])).start()
+        remote(0, send0.at[fars[a] * nnear + nears[b]], recv0.at[me], (fars[a], nears[b]), 3 * a).start()
     recv0[me] = send0[me]
 
     for load in gates:
         load.wait()
     put_high(0, tops_after_mids(0))
     put_high(1, tops_after_mids(2))
-    put_high(1, complex_rows(high_of(1), tops_after_mids(1)))
+    put_high(1, complex_rows(high_of(1), split(tops_after_mids(1))))
     put_high(2, tops_after_mids(3))
     put_high(3, tops_after_mids(4))
     put_high(4, tops_after_mids(6))
-    put_high(4, complex_rows(high_of(4), tops_after_mids(5)))
-
-    settle(recv0.at[pl.ds(0, nfar * nnear - 1)], recv_sem.at[0])
-    pair = tuple(recv0[:, c].reshape(rows, lows) for c in range(2))
-    pair = complex_rows(high_of(0), traded(pair, ((32, 32), (16, 16), (8, 8))))
-    pair = complex_rows(high_of(1), traded(pair, ((64, 32), (32, 16), (16, 8))))
-    pair = complex_rows(high_of(2), traded(pair, ((128, 4), (64, 2), (32, 1))))
-    for c in range(2):
-        for k in range(2):
-            send1[k, c] = pair[c][k * order : (k + 1) * order]
-    remote(1, send1.at[1 - core], recv1.at[core], (far, nears[1])).start()
-    recv1[core] = send1[core]
-    settle(recv1.at[0], recv_sem.at[1])
-
-    pair = tuple(recv1[:, c].reshape(rows, lows) for c in range(2))
-    pair = complex_rows(high_of(3), traded(pair, ((64, 64),)))
-    pair = complex_rows(high_of(4), traded(pair, ((64, 4), (32, 2), (16, 1))))
-    pair = traded(pair, ((16, 64),))
+    put_high(4, complex_rows(high_of(4), split(tops_after_mids(5))))
+
+    def keep(at, pair):
+        count = pair[0].shape[0]
+        place = pl.ds(pl.multiple_of(at * count, count), count)
+        x_ref[0, place], x_ref[1, place] = parts(jnp.concatenate(pair, axis=1))
+
+    for a in range(nfar):
+        landed = recv0.at[pl.ds(fars[a] * nnear, nnear - 1 if a == 0 else nnear)]
+        settle(landed, recv_sem.at[3 * a])
+        pair = tuple(recv0[pl.ds(fars[a] * nnear, nnear), c].reshape(rows // nfar, lows) for c in range(2))
+        keep(fars[a], traded(pair, ((32, 32), (16, 16), (8, 8))))
+    pair = complex_rows(high_of(0), (x_ref[0], x_ref[1]))
+    pair = complex_rows(high_of(1), split(traded(pair, ((64, 32), (32, 16), (16, 8)))))
+    ready = split(traded(pair, ((128, 4), (64, 2), (32, 1))))
+    send1[0], send1[1] = complex_rows(rows_of(2, 1 - core), ready)
+    remote(1, send1, recv1, (far, nears[1])).start()
+    keep(core, traded(complex_rows(rows_of(2, core), ready), ((64, 64),)))
+    settle(recv1, recv_sem.at[1])
+    keep(1 - core, traded((recv1[0], recv1[1]), ((64, 64),)))
+    pair = complex_rows(high_of(3), (x_ref[0], x_ref[1]))
+    ready = split(traded(pair, ((64, 4), (32, 2), (16, 1))))
     thin = rows // nnear // 2
-    for c in range(2):
-        for b in range(nnear):
-            for k in range(2):
-                at = (b * 2 + k) * thin
-                send2[k * nnear + b, c] = pair[c][at : at + thin]
     here = far * (nnear // 2) + near // 2
     same = side == core
-    for b in (6, 7, 4, 5, 2, 3, 1, 0):
-        for a in (1, 0):
-            to = (core * 2 + (far % 2 + a) % 2, nears[b])
-            copy = remote(2, send2.at[to[0] % 2 * nnear + to[1]], recv2.at[here], to)
-            if a + b:
-                copy.start()
-            else:
-                @pl.when(jnp.logical_not(same))
-                def _():
+    for h in (1, 0):
+        top = (near // 4 + h) % 2
+        pair = traded(complex_rows(rows_of(4, top), ready), ((16, 64),))
+        for c in range(2):
+            for b in range(nnear // 2):
+                for k in range(2):
+                    at = (b * 2 + k) * thin
+                    send2[k * nnear + top * (nnear // 2) + b, c] = pair[c][at : at + thin]
+        for b in (2, 3, 1, 0):
+            for a in (1, 0):
+                to = (core * 2 + (far % 2 + a) % 2, nears[4 * h + b])
+                copy = remote(2, send2.at[to[0] % 2 * nnear + to[1]], recv2.at[here], to)
+                if a + b + h:
                     copy.start()
-
-                @pl.when(same)
-                def _():
-                    recv2[here] = send2[far % 2 * nnear + near]
+                else:
+                    @pl.when(jnp.logical_not(same))
+                    def _():
+                        copy.start()
+
+                    @pl.when(same)
+                    def _():
+                        recv2[here] = send2[far % 2 * nnear + near]
 
     put_high(5, tops_after_mids(7))
     put_low(0, product(gate(5, 0), product(gate(4, 0), product(gate(3, 0), gate(2, 0)))), True)
@@ -355,10 +370,10 @@
         )
         for x in pair
     )
-    or_ref[...], oi_ref[...] = complex_rows(high_of(5), pair)
+    o_ref[0], o_ref[1] = complex_rows(high_of(5), split(pair))
 
     settle(send0.at[pl.ds(0, nfar * nnear - 1)], send_sem.at[0])
-    settle(send1.at[0], send_sem.at[1])
+    settle(send1, send_sem.at[1])
 
     @pl.when(same)
     def _():
@@ -375,18 +390,18 @@
     rows = high * order
     blocks = (
         (nfar * nnear, 2, rows // nfar // nnear, lows),
-        (2, 2, rows // 2, lows),
+        (2, rows // 2, lows),
         (2 * nnear, 2, rows // nnear // 2, lows),
     )
     buffers = [pltpu.VMEM(block, jnp.float32) for block in blocks]
     vmem = pl.BlockSpec(memory_space=pltpu.VMEM)
     anywhere = pl.BlockSpec(memory_space=pl.ANY)
     result = pltpu.VMEM((rows, lows), jnp.float32)
-    real, imag = pl.pallas_call(
+    both = pl.pallas_call(
         functools.partial(kernel, (nfar, nnear, high, order, lows)),
-        out_shape=(result, result),
+        out_shape=pltpu.VMEM((2, rows, lows), jnp.float32),
         in_specs=[anywhere] * 4,
-        out_specs=(vmem, vmem),
+        out_specs=vmem,
         scratch_shapes=[
             pltpu.VMEM((2, rows, lows), jnp.float32),
             pltpu.VMEM((2, order, order), jnp.float32),
@@ -400,8 +415,9 @@
         + buffers
         + buffers
         + [
+            pltpu.VMEM((2, rows, 2 * lows), jnp.bfloat16),
             pltpu.SemaphoreType.DMA((3,)),
-            pltpu.SemaphoreType.DMA((3,)),
+            pltpu.SemaphoreType.DMA((3 * nfar,)),
             pltpu.SemaphoreType.DMA((6,)),
         ],
         compiler_params=pltpu.CompilerParams(collective_id=0, has_side_effects=True),
@@ -411,7 +427,7 @@
         gate_real,
         gate_imag,
     )
-    return real.reshape(shape), imag.reshape(shape)
+    return both[0].reshape(shape), both[1].reshape(shape)
 
 
 def solution(mesh):

time: 31.2 us -> 30.3 us (0.971)
  local copies, waits for them, and re-layouts: 1.31 us -> 0.72 us
    unnamed x2 -> x0, local copies, waits for them, and re-layouts: 1.31 us -> none
    slice x0 -> x1, local copies, waits for them, and re-layouts: none -> 0.72 us  [one_kernel(): return (both[0].reshape(shape), both[1].reshape(shape))]
where the time goes in v4:
time: 30.3 us; the launch traced here: 30.1 us
  Pallas kernels  28.8 us (95%)
  local copies, waits for them, and re-layouts  0.72 us (2%)
  between operations  0.64 us (2%)
    pallas_call x1, Pallas kernels, one_kernel(): pl.pallas_call(functools.partial(kernel, (nfar, nnear, high, order, lows)...  28.8 us
    slice x1, local copies, waits for them, and re-layouts, one_kernel(): return (both[0].reshape(shape), both[1].reshape(shape))  0.72 us

profile of v4, /device:TPU:0, one launch (start us, length us, event | category | flops | bytes accessed | tf_op | source)
XLA Modules:
  0.0 30.1 jit_solution(8748490669237922109)
XLA Ops:
  0.6 28.8 %shard_map.59 = f32[2,256,128]{2,1,0:T(8,128)S(1)} custom-call(f32[256,128]{1,0:T(8,128)} %bitcast.4, f32[256,128]{1,0:T(8,128)} %bitcast.5, f32[2,4,3,128,128]{4,3,2,1,0:T(8,128)} %gr_hbm.1, f32[2,4,3,128,128]{4,3,2,1,0:T(8,128)} %gi_hbm.1), custom_call_target="tpu_custom_call" | custom-call | tf_op jit(solution)/shard_map/pallas_call | solution.py:400
  29.4 0.7 %fusion = (f32[1,256,128]{2,1,0:T(8,128)}, f32[1,256,128]{2,1,0:T(8,128)}) fusion(f32[2,256,128]{2,1,0:T(8,128)S(1)} %shard_map.59), kind=kLoop, calls=%fused_computation | loop fusion | bytes 524288 | tf_op jit(solution)/shard_map/slice | solution.py:430

commit v5 on v4

--- a/solution.py
+++ b/solution.py
@@ -164,10 +164,10 @@
     (
         st_ref, lr_ref, li_ref, gr_ref, gi_ref, kf_ref, km_ref, w_ref,
         send0, send1, send2, recv0, recv1, recv2,
-        x_ref, send_sem, recv_sem, load_sem,
+        x_ref, send_sem, recv_sem, load_sem, ready_sem,
     ) = scratch
     far, near = lax.axis_index("far"), lax.axis_index("near")
-    core, side = near % 2, far // 2
+    core, side = near % 2, far % 2
     upper = order // high
     rest = order // upper
     rows = high * order
@@ -185,7 +185,9 @@
     others.sort(key=lambda ab: -(ab[0] + ab[1] // 4 + ab[1] // 2 % 2))
 
     barrier = pltpu.get_barrier_semaphore()
-    for a, b in others:
+    close = [(a, b) for a, b in others if a * b == 0]
+    distant = [(a, b) for a, b in others if a * b]
+    for a, b in close:
         pl.semaphore_signal(
             barrier, inc=1, device_id=(fars[a], nears[b]), device_id_type=pl.DeviceIdType.MESH
         )
@@ -248,6 +250,14 @@
         places = [pl.ds(pl.multiple_of(half * order, order) + c * rows, order) for c in range(2)]
         return tuple(jnp.concatenate([km_ref[at, p, place] for place in places], axis=0) for p in range(2))
 
+    def rows_with(at, half):
+        places = [
+            pl.ds(pl.multiple_of(half * upper, upper) + (c * high + k) * order, upper)
+            for c in range(2)
+            for k in range(high)
+        ]
+        return tuple(jnp.concatenate([km_ref[at, p, place] for place in places], axis=0) for p in range(2))
+
     def put_low(at, pair, finely):
         wide = complex_matrix(*pair).T
         if finely:
@@ -285,10 +295,15 @@
             for k in range(fine):
                 at = (h * fine + k) * eight
                 send0[k * high + h, c] = pair[c][at : at + eight]
-    pl.semaphore_wait(barrier, nfar * nnear - 1)
+    pl.semaphore_wait(barrier, len(close))
+    for a in range(1, nfar):
+        pl.semaphore_signal(ready_sem, inc=1, device_id=(fars[a], near), device_id_type=pl.DeviceIdType.MESH)
     me = far * nnear + near
-    for a, b in others:
-        remote(0, send0.at[fars[a] * nnear + nears[b]], recv0.at[me], (fars[a], nears[b]), 3 * a).start()
+    for peers in (close, distant):
+        if peers is distant:
+            pl.semaphore_wait(ready_sem, nfar - 1)
+        for a, b in peers:
+            remote(0, send0.at[fars[a] * nnear + nears[b]], recv0.at[me], (fars[a], nears[b]), 3 * a).start()
     recv0[me] = send0[me]
 
     for load in gates:
@@ -314,9 +329,9 @@
     pair = complex_rows(high_of(0), (x_ref[0], x_ref[1]))
     pair = complex_rows(high_of(1), split(traded(pair, ((64, 32), (32, 16), (16, 8)))))
     ready = split(traded(pair, ((128, 4), (64, 2), (32, 1))))
-    send1[0], send1[1] = complex_rows(rows_of(2, 1 - core), ready)
+    send1[0], send1[1] = complex_rows(rows_with(2, 1 - core), ready)
     remote(1, send1, recv1, (far, nears[1])).start()
-    keep(core, traded(complex_rows(rows_of(2, core), ready), ((64, 64),)))
+    keep(core, traded(complex_rows(rows_with(2, core), ready), ((64, 64),)))
     settle(recv1, recv_sem.at[1])
     keep(1 - core, traded((recv1[0], recv1[1]), ((64, 64),)))
     pair = complex_rows(high_of(3), (x_ref[0], x_ref[1]))
@@ -334,8 +349,8 @@
                     send2[k * nnear + top * (nnear // 2) + b, c] = pair[c][at : at + thin]
         for b in (2, 3, 1, 0):
             for a in (1, 0):
-                to = (core * 2 + (far % 2 + a) % 2, nears[4 * h + b])
-                copy = remote(2, send2.at[to[0] % 2 * nnear + to[1]], recv2.at[here], to)
+                to = ((far // 2 + a) % 2 * 2 + core, nears[4 * h + b])
+                copy = remote(2, send2.at[to[0] // 2 * nnear + to[1]], recv2.at[here], to)
                 if a + b + h:
                     copy.start()
                 else:
@@ -345,7 +360,7 @@
 
                     @pl.when(same)
                     def _():
-                        recv2[here] = send2[far % 2 * nnear + near]
+                        recv2[here] = send2[far // 2 * nnear + near]
 
     put_high(5, tops_after_mids(7))
     put_low(0, product(gate(5, 0), product(gate(4, 0), product(gate(3, 0), gate(2, 0)))), True)
@@ -419,6 +434,7 @@
             pltpu.SemaphoreType.DMA((3,)),
             pltpu.SemaphoreType.DMA((3 * nfar,)),
             pltpu.SemaphoreType.DMA((6,)),
+            pltpu.SemaphoreType.REGULAR,
         ],
         compiler_params=pltpu.CompilerParams(collective_id=0, has_side_effects=True),
     )(

time: 30.3 us -> 29.5 us (0.974)
  Pallas kernels: 28.8 us -> 28 us
    pallas_call x1, Pallas kernels: 28.8 us -> 28 us  [one_kernel(): pl.pallas_call(functools.partial(kernel, (nfar, nnear, high, order, lows)...]
where the time goes in v5:
time: 29.5 us; the launch traced here: 29.4 us
  Pallas kernels  28 us (95%)
  local copies, waits for them, and re-layouts  0.72 us (2%)
  between operations  0.64 us (2%)
    pallas_call x1, Pallas kernels, one_kernel(): pl.pallas_call(functools.partial(kernel, (nfar, nnear, high, order, lows)...  28 us
    slice x1, local copies, waits for them, and re-layouts, one_kernel(): return (both[0].reshape(shape), both[1].reshape(shape))  0.72 us

profile of v5, /device:TPU:0, one launch (start us, length us, event | category | flops | bytes accessed | tf_op | source)
XLA Modules:
  0.0 29.4 jit_solution(12340411042018705567)
XLA Ops:
  0.6 28.0 %shard_map.59 = f32[2,256,128]{2,1,0:T(8,128)S(1)} custom-call(f32[256,128]{1,0:T(8,128)} %bitcast.4, f32[256,128]{1,0:T(8,128)} %bitcast.5, f32[2,4,3,128,128]{4,3,2,1,0:T(8,128)} %gr_hbm.1, f32[2,4,3,128,128]{4,3,2,1,0:T(8,128)} %gi_hbm.1), custom_call_target="tpu_custom_call" | custom-call | tf_op jit(solution)/shard_map/pallas_call | solution.py:415
  28.7 0.7 %fusion = (f32[1,256,128]{2,1,0:T(8,128)}, f32[1,256,128]{2,1,0:T(8,128)}) fusion(f32[2,256,128]{2,1,0:T(8,128)S(1)} %shard_map.59), kind=kLoop, calls=%fused_computation | loop fusion | bytes 524288 | tf_op jit(solution)/shard_map/slice | solution.py:446

commit v6 on v5

--- a/solution.py
+++ b/solution.py
@@ -164,7 +164,7 @@
     (
         st_ref, lr_ref, li_ref, gr_ref, gi_ref, kf_ref, km_ref, w_ref,
         send0, send1, send2, recv0, recv1, recv2,
-        x_ref, send_sem, recv_sem, load_sem, ready_sem,
+        x_ref, relay_ref, send_sem, recv_sem, load_sem, ready_sem,
     ) = scratch
     far, near = lax.axis_index("far"), lax.axis_index("near")
     core, side = near % 2, far % 2
@@ -184,6 +184,7 @@
     others = [(a, b) for a in range(nfar) for b in range(nnear) if a + b]
     others.sort(key=lambda ab: -(ab[0] + ab[1] // 4 + ab[1] // 2 % 2))
 
+    relayed = (1, 2)
     barrier = pltpu.get_barrier_semaphore()
     close = [(a, b) for a, b in others if a * b == 0]
     distant = [(a, b) for a, b in others if a * b]
@@ -204,12 +205,12 @@
     for load in first + gates:
         load.start()
 
-    def remote(stage, source, target, to, group=0):
+    def remote(stage, source, target, to, at):
         return pltpu.make_async_remote_copy(
             src_ref=source,
             dst_ref=target,
             send_sem=send_sem.at[stage],
-            recv_sem=recv_sem.at[stage + group],
+            recv_sem=recv_sem.at[at],
             device_id=to,
             device_id_type=pl.DeviceIdType.MESH,
         )
@@ -299,10 +300,15 @@
     for a in range(1, nfar):
         pl.semaphore_signal(ready_sem, inc=1, device_id=(fars[a], near), device_id_type=pl.DeviceIdType.MESH)
     me = far * nnear + near
-    for peers in (close, distant):
-        if peers is distant:
-            pl.semaphore_wait(ready_sem, nfar - 1)
-        for a, b in peers:
+    for a, b in close:
+        if a:
+            for i, k in enumerate(relayed):
+                block = send0.at[fars[a] * nnear + nears[k]]
+                remote(3, block, relay_ref.at[far, i], (fars[a], near), 1).start()
+        remote(0, send0.at[fars[a] * nnear + nears[b]], recv0.at[me], (fars[a], nears[b]), 3 * a).start()
+    pl.semaphore_wait(ready_sem, nfar - 1)
+    for a, b in distant:
+        if b not in relayed:
             remote(0, send0.at[fars[a] * nnear + nears[b]], recv0.at[me], (fars[a], nears[b]), 3 * a).start()
     recv0[me] = send0[me]
 
@@ -312,6 +318,10 @@
     put_high(1, tops_after_mids(2))
     put_high(1, complex_rows(high_of(1), split(tops_after_mids(1))))
     put_high(2, tops_after_mids(3))
+    settle(relay_ref.at[pl.ds(0, nfar - 1)], recv_sem.at[1])
+    for a in range(1, nfar):
+        for i, k in enumerate(relayed):
+            remote(3, relay_ref.at[fars[a], i], recv0.at[fars[a] * nnear + near], (far, nears[k]), 3 * a).start()
     put_high(3, tops_after_mids(4))
     put_high(4, tops_after_mids(6))
     put_high(4, complex_rows(high_of(4), split(tops_after_mids(5))))
@@ -330,9 +340,9 @@
     pair = complex_rows(high_of(1), split(traded(pair, ((64, 32), (32, 16), (16, 8)))))
     ready = split(traded(pair, ((128, 4), (64, 2), (32, 1))))
     send1[0], send1[1] = complex_rows(rows_with(2, 1 - core), ready)
-    remote(1, send1, recv1, (far, nears[1])).start()
+    remote(1, send1, recv1, (far, nears[1]), 2).start()
     keep(core, traded(complex_rows(rows_with(2, core), ready), ((64, 64),)))
-    settle(recv1, recv_sem.at[1])
+    settle(recv1, recv_sem.at[2])
     keep(1 - core, traded((recv1[0], recv1[1]), ((64, 64),)))
     pair = complex_rows(high_of(3), (x_ref[0], x_ref[1]))
     ready = split(traded(pair, ((64, 4), (32, 2), (16, 1))))
@@ -350,7 +360,7 @@
         for b in (2, 3, 1, 0):
             for a in (1, 0):
                 to = ((far // 2 + a) % 2 * 2 + core, nears[4 * h + b])
-                copy = remote(2, send2.at[to[0] // 2 * nnear + to[1]], recv2.at[here], to)
+                copy = remote(2, send2.at[to[0] // 2 * nnear + to[1]], recv2.at[here], to, 4)
                 if a + b + h:
                     copy.start()
                 else:
@@ -370,11 +380,11 @@
 
     @pl.when(same)
     def _():
-        settle(recv2.at[pl.ds(0, count - 1)], recv_sem.at[2])
+        settle(recv2.at[pl.ds(0, count - 1)], recv_sem.at[4])
 
     @pl.when(jnp.logical_not(same))
     def _():
-        settle(recv2, recv_sem.at[2])
+        settle(recv2, recv_sem.at[4])
 
     pair = tuple(recv2[:, c].reshape(rows, lows) for c in range(2))
     pair = low_gate(0, traded(pair, ((128, 64), (64, 4), (32, 2), (16, 1))))
@@ -387,7 +397,9 @@
     )
     o_ref[0], o_ref[1] = complex_rows(high_of(5), split(pair))
 
-    settle(send0.at[pl.ds(0, nfar * nnear - 1)], send_sem.at[0])
+    passed = (nfar - 1) * len(relayed)
+    settle(send0.at[pl.ds(0, nfar * nnear - 1 - passed)], send_sem.at[0])
+    settle(send0.at[pl.ds(0, 2 * passed)], send_sem.at[3])
     settle(send1, send_sem.at[1])
 
     @pl.when(same)
@@ -431,8 +443,9 @@
         + buffers
         + [
             pltpu.VMEM((2, rows, 2 * lows), jnp.bfloat16),
-            pltpu.SemaphoreType.DMA((3,)),
-            pltpu.SemaphoreType.DMA((3 * nfar,)),
+            pltpu.VMEM((nfar, 2) + blocks[0][1:], jnp.float32),
+            pltpu.SemaphoreType.DMA((4,)),
+            pltpu.SemaphoreType.DMA((3 * nfar - 2,)),
             pltpu.SemaphoreType.DMA((6,)),
             pltpu.SemaphoreType.REGULAR,
         ],

time: 29.5 us -> 29.1 us (0.986)
  Pallas kernels: 28 us -> 27.6 us
    pallas_call x1, Pallas kernels: 28 us -> 27.6 us  [one_kernel(): pl.pallas_call(functools.partial(kernel, (nfar, nnear, high, order, lows)...]
where the time goes in v6:
time: 29.1 us; the launch traced here: 29 us
  Pallas kernels  27.6 us (95%)
  local copies, waits for them, and re-layouts  0.72 us (2%)
  between operations  0.64 us (2%)
    pallas_call x1, Pallas kernels, one_kernel(): pl.pallas_call(functools.partial(kernel, (nfar, nnear, high, order, lows)...  27.6 us
    slice x1, local copies, waits for them, and re-layouts, one_kernel(): return (both[0].reshape(shape), both[1].reshape(shape))  0.72 us

profile of v6, /device:TPU:0, one launch (start us, length us, event | category | flops | bytes accessed | tf_op | source)
XLA Modules:
  0.0 29.0 jit_solution(4791778671944049778)
XLA Ops:
  0.6 27.6 %shard_map.59 = f32[2,256,128]{2,1,0:T(8,128)S(1)} custom-call(f32[256,128]{1,0:T(8,128)} %bitcast.4, f32[256,128]{1,0:T(8,128)} %bitcast.5, f32[2,4,3,128,128]{4,3,2,1,0:T(8,128)} %gr_hbm.1, f32[2,4,3,128,128]{4,3,2,1,0:T(8,128)} %gi_hbm.1), custom_call_target="tpu_custom_call" | custom-call | tf_op jit(solution)/shard_map/pallas_call | solution.py:427
  28.2 0.7 %fusion = (f32[1,256,128]{2,1,0:T(8,128)}, f32[1,256,128]{2,1,0:T(8,128)}) fusion(f32[2,256,128]{2,1,0:T(8,128)S(1)} %shard_map.59), kind=kLoop, calls=%fused_computation | loop fusion | bytes 524288 | tf_op jit(solution)/shard_map/slice | solution.py:459
